TPU v7x, 32 devices: a whole 2x2x4 slice. The times are simulated.
32 devices in a mesh: member: 8 (over y, x, core), lat: 4 (over z).
Axes of the slice: x: 2, y: 2, z: 4, core: 2. Of those that a mesh axis runs over, the one named last changes fastest.
Arguments:
- ensemble: float32 [16, 3, 1, 32, 1440], P('member', None, None, 'lat'), may hold values from -6 to 6
- observation: float32 [3, 1, 32, 1440], P(None, None, 'lat'), may hold values from -6 to 6
- valid_mask: int32 [16], P('member'), may hold values from 0 to 1, as said below
- band_start: int32 [4], P('lat'), may hold values from 0 to 713
Outputs:
- crps_field: float32 [3, 1, 32, 1440], P(None, None, ('lat', 'member'))
- score_table: float32 [3, 1], replicated
Inputs may be any that keep to these rules, and one draw needn't show every extreme that they name: `valid_mask`: exactly 13 entries are 1, at positions drawn afresh.
All inputs are finite; a program needn't handle non-finite values.
Results may differ from a plain program's by a relative error of at most 0.0001.
Values sent between devices are 32-bit elements; how exact they have to be, the bound alone decides.
A program may use at most 64 MiB of HBM per device.

v0:
```python
import functools
import math

import jax
import jax.numpy as jnp
from jax import lax
from jax.experimental import pallas as pl
from jax.experimental.pallas import tpu as pltpu
from jax.sharding import PartitionSpec as P

GRID_LAT = 721
GRID_LON = 1440
LANES = 128
SUBLANES = 8
FILL = 1e30
VMEM_BYTES = 67_043_328 - 65_536
MESH = pl.DeviceIdType.MESH


def round_up(value, step):
    return (value + step - 1) // step * step


def sort_pairs(count):
    pairs = []
    p = 1
    while p < count:
        k = p
        while k >= 1:
            for j in range(k % p, count - k, 2 * k):
                for i in range(min(k, count - j - k)):
                    if (i + j) // (2 * p) == (i + j + k) // (2 * p):
                        pairs.append((i + j, i + j + k))
            k //= 2
        p *= 2
    return pairs


def other(me, k, n):
    partner, bit = 0, 1
    while bit < n:
        here = (me // bit) % 2
        partner = partner + bit * (1 - here if k & bit else here)
        bit *= 2
    return partner


class Packing:
    def __init__(self, units, lon):
        self.units, self.full, self.tail = units, lon // LANES, lon % LANES
        self.beside = LANES // self.tail if self.tail else 1
        self.tails = round_up(units, self.beside) // self.beside if self.tail else 0
        self.lines = units * self.full + self.tails
        self.used = (units - 1) % self.beside * self.tail + self.tail

    def line(self, load, number):
        if number < self.units * self.full:
            return load(number // self.full, number % self.full * LANES, LANES)
        first = (number - self.units * self.full) * self.beside
        last = min(first + self.beside, self.units)
        parts = [load(u, self.full * LANES, self.tail) for u in range(first, last)]
        empty = LANES - self.tail * len(parts)
        if empty:
            parts.append(jnp.zeros((SUBLANES, empty), jnp.float32))
        return jnp.concatenate(parts, axis=1) if len(parts) > 1 else parts[0]

    def mask(self, unit, line, lane):
        inside = (line >= unit * self.full) & (line < (unit + 1) * self.full)
        if self.tail:
            low = unit % self.beside * self.tail
            at = self.units * self.full + unit // self.beside
            inside |= (line == at) & (lane >= low) & (lane < low + self.tail)
        return inside

    def pieces(self):
        for u in range(self.units):
            for c in range(self.full):
                yield u, c * LANES, LANES, u * self.full + c, 0
            if self.tail:
                at = self.units * self.full + u // self.beside
                yield u, self.full * LANES, self.tail, at, u % self.beside * self.tail


def kernel(
    n, nz, ens_ref, obs_ref, mask_ref, band_ref, field_ref, table_ref,
    ens_v, obs_v, mask_s, packet, obs_rows, gathered, partials,
    load_sem, send_sem, recv_sem, psend_sem, precv_sem, ready_sem,
):
    held, variables, leads, rows, lon = ens_ref.shape
    units = variables * leads
    packing = Packing(units, lon)
    lines = packing.lines
    pitch = packet.shape[0] // n
    stride = obs_rows.shape[0] // n
    slots = n * held
    total = n * nz
    me = lax.axis_index("member")
    band = lax.axis_index("lat")
    mine = band * n + me

    loads = [pltpu.make_async_copy(mask_ref, mask_s, load_sem.at[held + 1])]
    loads += [pltpu.make_async_copy(ens_ref.at[m], ens_v.at[m], load_sem.at[m]) for m in range(held)]
    loads.append(pltpu.make_async_copy(obs_ref, obs_v, load_sem.at[held]))
    plane = [{"member": other(me, k, n), "lat": band} for k in range(1, n)]
    line_peers = [{"member": me, "lat": lax.rem(band + k, nz)} for k in range(1, nz)]
    barrier = pltpu.get_barrier_semaphore()
    for peer in plane[::-1] + line_peers:
        pl.semaphore_signal(barrier, inc=1, device_id=peer, device_id_type=MESH)
    for load in loads:
        load.start()

    loads[0].wait()
    free = lax.broadcasted_iota(jnp.int32, (SUBLANES, LANES), 1) >= packing.used
    for m in range(held):
        loads[1 + m].wait()
        flag = jnp.full((SUBLANES, LANES), mask_s[m], jnp.int32)
        keep = flag != 0
        for block in range(0, rows, SUBLANES):
            base = block * pitch

            def load(u, low, wide):
                return ens_v[m, u // leads, u % leads, pl.ds(block, SUBLANES), pl.ds(low, wide)]

            for line in range(lines):
                value = jnp.where(keep, packing.line(load, line), FILL)
                if line == lines - 1:
                    value = jnp.where(free, flag.astype(jnp.float32), value)
                packet[pl.ds(base + m * lines + line, SUBLANES, stride=pitch), :] = value
            for line in range(held * lines + m, pitch, held):
                packet[pl.ds(base + line, SUBLANES, stride=pitch), :] = jnp.zeros_like(value)

    pl.semaphore_wait(barrier, n - 1 + nz - 1)

    sends = []
    for k in sorted(range(1, n), key=lambda k: (-bin(k // 2).count("1"), k)):
        sends.append(
            pltpu.make_async_remote_copy(
                src_ref=packet.at[
                    pl.ds(pl.multiple_of(plane[k - 1]["member"] * pitch, SUBLANES), held * lines)
                ],
                dst_ref=gathered.at[
                    pl.ds(pl.multiple_of(me * pitch, SUBLANES), held * lines)
                ],
                send_sem=send_sem.at[k],
                recv_sem=recv_sem.at[k],
                device_id=plane[k - 1],
                device_id_type=MESH,
            )
        )
        sends[-1].start()
    for peer in line_peers:
        pl.semaphore_signal(ready_sem, inc=1, device_id=peer, device_id_type=MESH)

    loads[1 + held].wait()
    for block in range(0, rows, SUBLANES):

        def load(u, low, wide):
            return obs_v[u // leads, u % leads, pl.ds(block, SUBLANES), pl.ds(low, wide)]

        for line in range(lines):
            obs_rows[pl.ds(block * stride + line, SUBLANES, stride=stride), :] = packing.line(
                load, line
            )
    gathered[pl.ds(pl.multiple_of(me * pitch, SUBLANES), pitch), :] = packet[
        pl.ds(pl.multiple_of(me * pitch, SUBLANES), pitch), :
    ]
    row_number = jnp.full((1, LANES), band_ref[0] + me, jnp.int32).astype(jnp.float32)
    weight = jnp.cos((90.0 - row_number * 180.0 / (GRID_LAT - 1)) * math.pi / 180.0)
    pl.semaphore_wait(ready_sem, nz - 1)

    for send in sends:
        send.wait_recv()

    flags = jnp.concatenate(
        [
            gathered[pl.ds(s // held * pitch + s % held * lines + lines - 1, 1), :]
            for s in range(slots)
        ],
        axis=0,
    )
    count = jnp.sum(flags, axis=0, keepdims=True)
    count = jnp.where(free[:1], count, 0.0)
    count = jnp.max(count, axis=1, keepdims=True)
    count = jnp.broadcast_to(count, (SUBLANES, LANES))
    per_one = 1.0 / count
    per_pair = per_one / (count - 1.0)
    skill_weight, spread_weight = [], []
    for i in range(slots):
        counted = i < count
        skill_weight.append(jnp.where(counted, per_one, 0.0))
        spread_weight.append(jnp.where(counted, (2.0 * i + 1.0 - count) * per_pair, 0.0))

    network = sort_pairs(slots)
    sums = [None] * units
    blocks = []
    lane = lax.broadcasted_iota(jnp.int32, (SUBLANES, LANES), 1)
    for j in range(0, lines, SUBLANES):
        x = [
            gathered[pl.ds(s // held * pitch + s % held * lines + j, SUBLANES), :]
            for s in range(slots)
        ]
        for a, b in network:
            x[a], x[b] = jnp.minimum(x[a], x[b]), jnp.maximum(x[a], x[b])
        truth = obs_rows[pl.ds(pl.multiple_of(me * stride + j, SUBLANES), SUBLANES), :]
        score = None
        for i in range(slots):
            term = skill_weight[i] * jnp.abs(x[i] - truth) - spread_weight[i] * x[i]
            score = term if score is None else score + term
        blocks.append(score)
        line = j + lax.broadcasted_iota(jnp.int32, (SUBLANES, LANES), 0)
        for u in range(units):
            part = jnp.where(packing.mask(u, line, lane), score, 0.0)
            sums[u] = part if sums[u] is None else sums[u] + part

    lane = lax.broadcasted_iota(jnp.int32, (1, LANES), 1)
    row = jnp.zeros((1, LANES), jnp.float32)
    for u in range(units):
        one = jnp.sum(jnp.sum(sums[u], axis=0, keepdims=True), axis=1, keepdims=True)
        row = jnp.where(lane == u, one, row)
    partials[pl.ds(mine, 1), :] = row * weight

    def share_with(far):
        return pltpu.make_async_remote_copy(
            src_ref=partials.at[pl.ds(mine, 1)],
            dst_ref=partials.at[pl.ds(mine, 1)],
            send_sem=psend_sem.at[far],
            recv_sem=precv_sem.at[mine],
            device_id={"member": far % n, "lat": far // n},
            device_id_type=MESH,
        )

    def share_from(far):
        return pltpu.make_async_remote_copy(
            src_ref=partials.at[pl.ds(mine, 1)],
            dst_ref=partials.at[pl.ds(far, 1)],
            send_sem=psend_sem.at[far],
            recv_sem=precv_sem.at[far],
            device_id={"member": far % n, "lat": far // n},
            device_id_type=MESH,
        )

    for far in range(total):
        pl.when(far != mine)(lambda far=far: share_with(far).start())

    for u, low, wide, at, first in packing.pieces():
        piece = blocks[at // SUBLANES][at % SUBLANES : at % SUBLANES + 1, first : first + wide]
        field_ref[u // leads, u % leads, :, pl.ds(low, wide)] = piece

    for send in sends:
        send.wait_send()
    for far in range(total):
        pl.when(far != mine)(lambda far=far: share_with(far).wait_send())
    for far in range(total):
        pl.when(far != mine)(lambda far=far: share_from(far).wait_recv())
    summed = jnp.sum(partials[...], axis=0, keepdims=True)
    table_ref[...] = summed[:, :units] / (nz * rows * GRID_LON)


def write_out(field_ref, table_ref, field_out, table_out, sem):
    copies = [
        pltpu.make_async_copy(field_ref, field_out, sem.at[0]),
        pltpu.make_async_copy(table_ref, table_out, sem.at[1]),
    ]
    for copy in copies:
        copy.start()
    for copy in copies:
        copy.wait()


def on_device(n, nz, ensemble, observation, valid_mask, band_start):
    held, variables, leads, rows, lon = ensemble.shape
    assert rows == n and rows % SUBLANES == 0
    units = variables * leads
    packing = Packing(units, lon)
    assert packing.tails and packing.used < LANES
    pitch = round_up(held * packing.lines, SUBLANES)
    stride = round_up(packing.lines, SUBLANES)
    total = n * nz
    field, table = pl.pallas_call(
        functools.partial(kernel, n, nz),
        out_shape=(
            pltpu.VMEM((variables, leads, rows // n, lon), jnp.float32),
            pltpu.VMEM((1, units), jnp.float32),
        ),
        in_specs=[pl.BlockSpec(memory_space=pltpu.HBM)] * 3 + [pl.BlockSpec(memory_space=pltpu.SMEM)],
        out_specs=(
            pl.BlockSpec(memory_space=pltpu.VMEM),
            pl.BlockSpec(memory_space=pltpu.VMEM),
        ),
        scratch_shapes=[
            pltpu.VMEM(ensemble.shape, jnp.float32),
            pltpu.VMEM(observation.shape, jnp.float32),
            pltpu.SMEM(valid_mask.shape, jnp.int32),
            pltpu.VMEM((n * pitch, LANES), jnp.float32),
            pltpu.VMEM((n * stride, LANES), jnp.float32),
            pltpu.VMEM((n * pitch + SUBLANES, LANES), jnp.float32),
            pltpu.VMEM((total, LANES), jnp.float32),
            pltpu.SemaphoreType.DMA((held + 2,)),
            pltpu.SemaphoreType.DMA((n,)),
            pltpu.SemaphoreType.DMA((n,)),
            pltpu.SemaphoreType.DMA((total,)),
            pltpu.SemaphoreType.DMA((total,)),
            pltpu.SemaphoreType.REGULAR,
        ],
        compiler_params=pltpu.CompilerParams(
            collective_id=0, has_side_effects=True, vmem_limit_bytes=VMEM_BYTES
        ),
        name="fair_crps",
    )(ensemble, observation, valid_mask, band_start)
    field, table = pl.pallas_call(
        write_out,
        out_shape=(
            jax.ShapeDtypeStruct(field.shape, jnp.float32),
            jax.ShapeDtypeStruct(table.shape, jnp.float32),
        ),
        in_specs=[pl.BlockSpec(memory_space=pltpu.VMEM)] * 2,
        out_specs=(pl.BlockSpec(memory_space=pltpu.HBM),) * 2,
        scratch_shapes=[pltpu.SemaphoreType.DMA((2,))],
        name="write_out",
    )(*(pltpu.with_memory_space_constraint(a, pltpu.VMEM) for a in (field, table)))
    return field, table.reshape(variables, leads)


def solution(mesh):
    placed = (
        P("member", None, None, "lat", None),
        P(None, None, "lat", None),
        P("member"),
        P("lat"),
    )
    return jax.shard_map(
        functools.partial(on_device, mesh.shape["member"], mesh.shape["lat"]),
        mesh=mesh,
        in_specs=placed,
        out_specs=(P(None, None, ("lat", "member"), None), P()),
        check_vma=False,
    )
```

profile of v0, /device:TPU:0, one launch (start us, length us, event | category | flops | bytes accessed | tf_op | source)
XLA Modules:
  0.0 17.4 jit_solution(15030007093115850378)
XLA Ops:
  1.3 15.5 %fair_crps.1 = (f32[3,1,1,1440]{3,2,1,0:T(1,128)S(1)}, f32[1,3]{1,0:T(1,128)S(1)}) custom-call(f32[2,3,1,8,1440]{4,3,2,1,0:T(8,128)} %ens_ref.1, f32[3,1,8,1440]{3,2,1,0:T(8,128)} %obs_ref.1, s32[2]{0:T(128)} %mask_ref.1, s32[1]{0:T(128)S(6)} %copy.6.band_ref), custom_call_target="tpu_custom_call" | custom-call | tf_op jit(solution)/shard_map/fair_crps/pallas_call | solution.py:279
  16.8 0.6 %write_out.1 = (f32[3,1,1,1440]{3,2,1,0:T(1,128)}, f32[1,3]{1,0:T(1,128)}) custom-call(f32[3,1,1,1440]{3,2,1,0:T(1,128)S(1)} %get-tuple-element.6.field_ref, f32[1,3]{1,0:T(1,128)S(1)} %get-tuple-element.7.table_ref), custom_call_target="tpu_custom_call" | custom-call | tf_op jit(solution)/shard_map/write_out/pallas_call | solution.py:310
where the time goes:
time: 17.5 us; the launch traced here: 17.4 us
  Pallas kernels  16.1 us (92%)
  between operations  1.28 us (7%)
    pallas_call x1, Pallas kernels, on_device(): pl.pallas_call(functools.partial(kernel, n, nz), out_shape=(pltpu.VMEM((v...  15.5 us
    pallas_call x1, Pallas kernels, on_device(): pl.pallas_call(write_out, out_shape=(jax.ShapeDtypeStruct(field.shape, jn...  0.63 us

commit v1 on v0

--- a/solution.py
+++ b/solution.py
@@ -223,8 +223,8 @@
         return pltpu.make_async_remote_copy(
             src_ref=partials.at[pl.ds(mine, 1)],
             dst_ref=partials.at[pl.ds(mine, 1)],
-            send_sem=psend_sem.at[far],
-            recv_sem=precv_sem.at[mine],
+            send_sem=psend_sem.at[0],
+            recv_sem=precv_sem.at[0],
             device_id={"member": far % n, "lat": far // n},
             device_id_type=MESH,
         )
@@ -233,8 +233,8 @@
         return pltpu.make_async_remote_copy(
             src_ref=partials.at[pl.ds(mine, 1)],
             dst_ref=partials.at[pl.ds(far, 1)],
-            send_sem=psend_sem.at[far],
-            recv_sem=precv_sem.at[far],
+            send_sem=psend_sem.at[0],
+            recv_sem=precv_sem.at[0],
             device_id={"member": far % n, "lat": far // n},
             device_id_type=MESH,
         )
@@ -248,10 +248,10 @@
 
     for send in sends:
         send.wait_send()
-    for far in range(total):
-        pl.when(far != mine)(lambda far=far: share_with(far).wait_send())
-    for far in range(total):
-        pl.when(far != mine)(lambda far=far: share_from(far).wait_recv())
+    everything = pltpu.make_async_copy(partials.at[pl.ds(1, total - 1)], partials.at[pl.ds(1, total - 1)], psend_sem.at[0])
+    everything.wait()
+    everything = pltpu.make_async_copy(partials.at[pl.ds(1, total - 1)], partials.at[pl.ds(1, total - 1)], precv_sem.at[0])
+    everything.wait()
     summed = jnp.sum(partials[...], axis=0, keepdims=True)
     table_ref[...] = summed[:, :units] / (nz * rows * GRID_LON)
 
@@ -298,8 +298,8 @@
             pltpu.SemaphoreType.DMA((held + 2,)),
             pltpu.SemaphoreType.DMA((n,)),
             pltpu.SemaphoreType.DMA((n,)),
-            pltpu.SemaphoreType.DMA((total,)),
-            pltpu.SemaphoreType.DMA((total,)),
+            pltpu.SemaphoreType.DMA((1,)),
+            pltpu.SemaphoreType.DMA((1,)),
             pltpu.SemaphoreType.REGULAR,
         ],
         compiler_params=pltpu.CompilerParams(

time: 17.5 us -> 17 us (0.971)
  Pallas kernels: 16.1 us -> 15.5 us
    pallas_call x1, Pallas kernels: 15.5 us -> 14.9 us  [on_device(): pl.pallas_call(functools.partial(kernel, n, nz), out_shape=(pltpu.VMEM((v...]
where the time goes in v1:
time: 17 us; the launch traced here: 16.8 us
  Pallas kernels  15.5 us (91%)
  between operations  1.28 us (8%)
    pallas_call x1, Pallas kernels, on_device(): pl.pallas_call(functools.partial(kernel, n, nz), out_shape=(pltpu.VMEM((v...  14.9 us
    pallas_call x1, Pallas kernels, on_device(): pl.pallas_call(write_out, out_shape=(jax.ShapeDtypeStruct(field.shape, jn...  0.63 us

profile of v1, /device:TPU:0, one launch (start us, length us, event | category | flops | bytes accessed | tf_op | source)
XLA Modules:
  0.0 16.8 jit_solution(15519572901416485414)
XLA Ops:
  1.3 14.9 %fair_crps.1 = (f32[3,1,1,1440]{3,2,1,0:T(1,128)S(1)}, f32[1,3]{1,0:T(1,128)S(1)}) custom-call(f32[2,3,1,8,1440]{4,3,2,1,0:T(8,128)} %ens_ref.1, f32[3,1,8,1440]{3,2,1,0:T(8,128)} %obs_ref.1, s32[2]{0:T(128)} %mask_ref.1, s32[1]{0:T(128)S(6)} %copy.6.band_ref), custom_call_target="tpu_custom_call" | custom-call | tf_op jit(solution)/shard_map/fair_crps/pallas_call | solution.py:279
  16.2 0.6 %write_out.1 = (f32[3,1,1,1440]{3,2,1,0:T(1,128)}, f32[1,3]{1,0:T(1,128)}) custom-call(f32[3,1,1,1440]{3,2,1,0:T(1,128)S(1)} %get-tuple-element.6.field_ref, f32[1,3]{1,0:T(1,128)S(1)} %get-tuple-element.7.table_ref), custom_call_target="tpu_custom_call" | custom-call | tf_op jit(solution)/shard_map/write_out/pallas_call | solution.py:310

commit v2 on v1

v2 whole, which is shorter than its diff:
```python
import functools
import math

import jax
import jax.numpy as jnp
from jax import lax
from jax.experimental import pallas as pl
from jax.experimental.pallas import tpu as pltpu
from jax.sharding import PartitionSpec as P

GRID_LAT = 721
LANES = 128
SUBLANES = 8
VMEM_BYTES = 67_043_328 - 65_536
MESH = pl.DeviceIdType.MESH


def round_up(value, step):
    return (value + step - 1) // step * step


def sort_pairs(count):
    pairs = []
    p = 1
    while p < count:
        k = p
        while k >= 1:
            for j in range(k % p, count - k, 2 * k):
                for i in range(min(k, count - j - k)):
                    if (i + j) // (2 * p) == (i + j + k) // (2 * p):
                        pairs.append((i + j, i + j + k))
            k //= 2
        p *= 2
    return pairs


def other(me, k, n):
    partner, bit = 0, 1
    while bit < n:
        here = (me // bit) % 2
        partner = partner + bit * (1 - here if k & bit else here)
        bit *= 2
    return partner


def steps(pair):
    return bin(pair).count("1")


class Packing:
    def __init__(self, units, lon):
        self.units, self.full, self.tail = units, lon // LANES, lon % LANES
        self.beside = LANES // self.tail if self.tail else 1
        self.tails = round_up(units, self.beside) // self.beside if self.tail else 0
        self.lines = units * self.full + self.tails
        self.used = (units - 1) % self.beside * self.tail + self.tail

    def line(self, load, number):
        if number >= self.tails:
            number -= self.tails
            return load(number // self.full, number % self.full * LANES, LANES)
        first = number * self.beside
        last = min(first + self.beside, self.units)
        parts = [load(u, self.full * LANES, self.tail) for u in range(first, last)]
        empty = LANES - self.tail * len(parts)
        if empty:
            parts.append(jnp.zeros((SUBLANES, empty), jnp.float32))
        return jnp.concatenate(parts, axis=1) if len(parts) > 1 else parts[0]

    def mask(self, unit, line, lane):
        start = self.tails + unit * self.full
        inside = (line >= start) & (line < start + self.full)
        if self.tail:
            low = unit % self.beside * self.tail
            inside |= (line == unit // self.beside) & (lane >= low) & (lane < low + self.tail)
        return inside

    def pieces(self):
        for u in range(self.units):
            for c in range(self.full):
                yield u, c * LANES, LANES, self.tails + u * self.full + c, 0
            if self.tail:
                yield u, self.full * LANES, self.tail, u // self.beside, u % self.beside * self.tail


class Layout:
    def __init__(self, held, lines):
        self.held, self.lines = held, lines
        self.split = max(lines // SUBLANES - 1, 1) * SUBLANES
        self.pitch = round_up(held * lines, SUBLANES)
        self.chunks = [(0, held * self.split), (held * self.split, held * (lines - self.split))]

    def row(self, m, line):
        if line < self.split:
            return m * self.split + line
        return self.held * self.split + m * (self.lines - self.split) + line - self.split


def kernel(
    n, nz, ens_ref, obs_ref, mask_ref, band_ref, field_ref, table_ref,
    ens_v, obs_v, mask_s, packet, obs_rows, gathered, partials,
    load_sem, send_sem, recv_sem, share_sem, wave_sem,
):
    held, variables, leads, rows, lon = ens_ref.shape
    units = variables * leads
    packing = Packing(units, lon)
    lines = packing.lines
    layout = Layout(held, lines)
    pitch, split = layout.pitch, layout.split
    stride = obs_rows.shape[0] // n
    slots = n * held
    total = n * nz
    me = lax.axis_index("member")
    band = lax.axis_index("lat")
    mine = band * n + me
    flag_line = packing.tails - 1

    plane = [{"member": other(me, k, n), "lat": band} for k in range(1, n)]
    above = {"member": me, "lat": lax.rem(band + 1, nz)}
    below = {"member": me, "lat": lax.rem(band + nz - 1, nz)}
    has_above = band < nz - 1
    has_below = band > 0

    def signal(sem, peer):
        pl.semaphore_signal(sem, inc=1, device_id=peer, device_id_type=MESH)

    barrier = pltpu.get_barrier_semaphore()
    for peer in plane[::-1]:
        signal(barrier, peer)
    mask_load = pltpu.make_async_copy(mask_ref, mask_s, load_sem.at[held + 1])
    ens_loads = [pltpu.make_async_copy(ens_ref.at[m], ens_v.at[m], load_sem.at[m]) for m in range(held)]
    obs_load = pltpu.make_async_copy(obs_ref, obs_v, load_sem.at[held])
    for load in [obs_load, mask_load] + ens_loads:
        load.start()
    pl.when(has_above)(lambda: signal(barrier, above))
    pl.when(has_below)(lambda: signal(barrier, below))

    mask_load.wait()
    obs_load.wait()
    free = lax.broadcasted_iota(jnp.int32, (SUBLANES, LANES), 1) >= packing.used

    def obs_line(block, line):
        def load(u, low, wide):
            return obs_v[u // leads, u % leads, pl.ds(block, SUBLANES), pl.ds(low, wide)]

        return packing.line(load, line)

    def pack(m, which):
        flag = jnp.full((SUBLANES, LANES), mask_s[m], jnp.int32)
        keep = flag != 0
        for block in range(0, rows, SUBLANES):

            def load(u, low, wide):
                return ens_v[m, u // leads, u % leads, pl.ds(block, SUBLANES), pl.ds(low, wide)]

            for line in which:
                value = jnp.where(keep, packing.line(load, line), obs_line(block, line))
                if line == flag_line:
                    value = jnp.where(free, flag.astype(jnp.float32), value)
                at = block * pitch + layout.row(m, line)
                packet[pl.ds(at, SUBLANES, stride=pitch), :] = value

    def send(chunk, to):
        low, size = layout.chunks[chunk]
        pltpu.make_async_remote_copy(
            src_ref=packet.at[pl.ds(to * pitch + low, size)],
            dst_ref=gathered.at[pl.ds(pl.multiple_of(me * pitch + low, SUBLANES), size)],
            send_sem=send_sem,
            recv_sem=recv_sem.at[chunk],
            device_id={"member": to, "lat": band},
            device_id_type=MESH,
        ).start()

    for m in range(held):
        ens_loads[m].wait()
        pack(m, range(lines))
    count_near = n - 1 + (band + nz - 1) // nz + (2 * nz - 2 - band) // nz
    pl.semaphore_wait(barrier, count_near)
    for to in sorted(range(n), key=lambda to: (-steps(to // 2), to)):

        @pl.when(to != me)
        def both(to=to):
            send(0, to)
            send(1, to)

    pl.when(band == nz - 1)(lambda: signal(wave_sem.at[1], below))
    for block in range(0, rows, SUBLANES):
        for line in range(lines):
            obs_rows[pl.ds(block * stride + line, SUBLANES, stride=stride), :] = obs_line(block, line)
    own = pl.ds(pl.multiple_of(me * pitch, SUBLANES), pitch)
    gathered[own, :] = packet[own, :]
    pl.when(has_below)(lambda: pl.semaphore_wait(wave_sem.at[0], 1))
    pl.when(has_above)(lambda: signal(wave_sem.at[0], above))
    row_number = jnp.full((1, LANES), band_ref[0] + me, jnp.int32).astype(jnp.float32)
    weight = jnp.cos((90.0 - row_number * 180.0 / (GRID_LAT - 1)) * math.pi / 180.0)
    pl.when(has_above)(lambda: pl.semaphore_wait(wave_sem.at[1], 1))
    pl.when(has_above & has_below)(lambda: signal(wave_sem.at[1], below))

    def arrived(sem, ref, size):
        whole = ref.at[pl.ds(0, size)]
        pltpu.make_async_copy(whole, whole, sem).wait()

    network = sort_pairs(slots)
    lane = lax.broadcasted_iota(jnp.int32, (SUBLANES, LANES), 1)
    below_line = lax.broadcasted_iota(jnp.int32, (SUBLANES, LANES), 0)
    sums = [None] * units
    per_skill = per_spread = None
    arrived(recv_sem.at[0], gathered, (n - 1) * layout.chunks[0][1])
    for j in range(0, lines, SUBLANES):
        if j == split:
            arrived(recv_sem.at[1], gathered, (n - 1) * layout.chunks[1][1])
        x = [
            gathered[pl.ds(s // held * pitch + layout.row(s % held, j), SUBLANES), :]
            for s in range(slots)
        ]
        if j == 0:
            flags = functools.reduce(jnp.add, x)
            flags = jnp.where((below_line == flag_line) & free, flags, 0.0)
            count = jnp.max(jnp.max(flags, axis=0, keepdims=True), axis=1, keepdims=True)
            count = jnp.broadcast_to(count, (SUBLANES, LANES))
            per_one = 1.0 / count
            per_spread = per_one / (count - 1.0)
            per_skill = per_one + (slots - count) * per_spread
        truth = obs_rows[pl.ds(pl.multiple_of(me * stride + j, SUBLANES), SUBLANES), :]
        skill = functools.reduce(jnp.add, [jnp.abs(value - truth) for value in x])
        for a, b in network:
            x[a], x[b] = jnp.minimum(x[a], x[b]), jnp.maximum(x[a], x[b])
        spread = functools.reduce(
            jnp.add,
            [(slots - 1.0 - 2.0 * i) * (x[slots - 1 - i] - x[i]) for i in range(slots // 2)],
        )
        score = per_skill * skill - per_spread * spread
        for u, low, wide, at, first in packing.pieces():
            if j <= at < j + SUBLANES:
                piece = score[at - j : at - j + 1, first : first + wide]
                field_ref[u // leads, u % leads, :, pl.ds(low, wide)] = piece
        for u in range(units):
            part = jnp.where(packing.mask(u, below_line + j, lane), score, 0.0)
            sums[u] = part if sums[u] is None else sums[u] + part

    lane = lax.broadcasted_iota(jnp.int32, (1, LANES), 1)
    row = jnp.zeros((1, LANES), jnp.float32)
    for u in range(units):
        one = jnp.sum(jnp.sum(sums[u], axis=0, keepdims=True), axis=1, keepdims=True)
        row = jnp.where(lane == u, one, row)
    partials[pl.ds(mine, 1), :] = row * weight

    def share_with(far):
        return pltpu.make_async_remote_copy(
            src_ref=partials.at[pl.ds(mine, 1)],
            dst_ref=partials.at[pl.ds(mine, 1)],
            send_sem=share_sem.at[0],
            recv_sem=share_sem.at[1],
            device_id={"member": far % n, "lat": far // n},
            device_id_type=MESH,
        )

    for far in range(total):
        pl.when(far != mine)(lambda far=far: share_with(far).start())
    arrived(send_sem, packet, (n - 1) * held * lines)
    arrived(share_sem.at[0], partials, total - 1)
    arrived(share_sem.at[1], partials, total - 1)
    summed = jnp.sum(partials[...], axis=0, keepdims=True)
    table_ref[...] = summed[:, :units] / (nz * rows * lon)


def write_out(field_ref, table_ref, field_out, table_out, sem):
    copies = [
        pltpu.make_async_copy(field_ref, field_out, sem.at[0]),
        pltpu.make_async_copy(table_ref, table_out, sem.at[1]),
    ]
    for copy in copies:
        copy.start()
    for copy in copies:
        copy.wait()


def on_device(n, nz, ensemble, observation, valid_mask, band_start):
    held, variables, leads, rows, lon = ensemble.shape
    assert rows == n and rows % SUBLANES == 0
    units = variables * leads
    packing = Packing(units, lon)
    assert packing.tails and packing.used < LANES
    assert n % 2 == 0 and packing.lines >= 2 * SUBLANES
    pitch = Layout(held, packing.lines).pitch
    stride = round_up(packing.lines, SUBLANES)
    total = n * nz
    field, table = pl.pallas_call(
        functools.partial(kernel, n, nz),
        out_shape=(
            pltpu.VMEM((variables, leads, rows // n, lon), jnp.float32),
            pltpu.VMEM((1, units), jnp.float32),
        ),
        in_specs=[pl.BlockSpec(memory_space=pltpu.HBM)] * 3 + [pl.BlockSpec(memory_space=pltpu.SMEM)],
        out_specs=(
            pl.BlockSpec(memory_space=pltpu.VMEM),
            pl.BlockSpec(memory_space=pltpu.VMEM),
        ),
        scratch_shapes=[
            pltpu.VMEM(ensemble.shape, jnp.float32),
            pltpu.VMEM(observation.shape, jnp.float32),
            pltpu.SMEM(valid_mask.shape, jnp.int32),
            pltpu.VMEM((n * pitch, LANES), jnp.float32),
            pltpu.VMEM((n * stride, LANES), jnp.float32),
            pltpu.VMEM((n * pitch + SUBLANES, LANES), jnp.float32),
            pltpu.VMEM((total, LANES), jnp.float32),
            pltpu.SemaphoreType.DMA((held + 2,)),
            pltpu.SemaphoreType.DMA,
            pltpu.SemaphoreType.DMA((2,)),
            pltpu.SemaphoreType.DMA((2,)),
            pltpu.SemaphoreType.REGULAR((2,)),
        ],
        compiler_params=pltpu.CompilerParams(
            collective_id=0, has_side_effects=True, vmem_limit_bytes=VMEM_BYTES
        ),
        name="fair_crps",
    )(ensemble, observation, valid_mask, band_start)
    field, table = pl.pallas_call(
        write_out,
        out_shape=(
            jax.ShapeDtypeStruct(field.shape, jnp.float32),
            jax.ShapeDtypeStruct(table.shape, jnp.float32),
        ),
        in_specs=[pl.BlockSpec(memory_space=pltpu.VMEM)] * 2,
        out_specs=(pl.BlockSpec(memory_space=pltpu.HBM),) * 2,
        scratch_shapes=[pltpu.SemaphoreType.DMA((2,))],
        name="write_out",
    )(*(pltpu.with_memory_space_constraint(a, pltpu.VMEM) for a in (field, table)))
    return field, table.reshape(variables, leads)


def solution(mesh):
    placed = (
        P("member", None, None, "lat", None),
        P(None, None, "lat", None),
        P("member"),
        P("lat"),
    )
    return jax.shard_map(
        functools.partial(on_device, mesh.shape["member"], mesh.shape["lat"]),
        mesh=mesh,
        in_specs=placed,
        out_specs=(P(None, None, ("lat", "member"), None), P()),
        check_vma=False,
    )
```

time: 17 us -> 16.6 us (0.976)
  Pallas kernels: 15.5 us -> 15.1 us
    pallas_call x1, Pallas kernels: 14.9 us -> 14.5 us  [on_device(): pl.pallas_call(functools.partial(kernel, n, nz), out_shape=(pltpu.VMEM((v...]
where the time goes in v2:
time: 16.6 us; the launch traced here: 16.4 us
  Pallas kernels  15.1 us (91%)
  between operations  1.28 us (8%)
    pallas_call x1, Pallas kernels, on_device(): pl.pallas_call(functools.partial(kernel, n, nz), out_shape=(pltpu.VMEM((v...  14.5 us
    pallas_call x1, Pallas kernels, on_device(): pl.pallas_call(write_out, out_shape=(jax.ShapeDtypeStruct(field.shape, jn...  0.63 us

profile of v2, /device:TPU:0, one launch (start us, length us, event | category | flops | bytes accessed | tf_op | source)
XLA Modules:
  0.0 16.4 jit_solution(12976343216981779001)
XLA Ops:
  1.3 14.5 %fair_crps.1 = (f32[3,1,1,1440]{3,2,1,0:T(1,128)S(1)}, f32[1,3]{1,0:T(1,128)S(1)}) custom-call(f32[2,3,1,8,1440]{4,3,2,1,0:T(8,128)} %ens_ref.1, f32[3,1,8,1440]{3,2,1,0:T(8,128)} %obs_ref.1, s32[2]{0:T(128)} %mask_ref.1, s32[1]{0:T(128)S(6)} %copy.6.band_ref), custom_call_target="tpu_custom_call" | custom-call | tf_op jit(solution)/shard_map/fair_crps/pallas_call | solution.py:288
  15.8 0.6 %write_out.1 = (f32[3,1,1,1440]{3,2,1,0:T(1,128)}, f32[1,3]{1,0:T(1,128)}) custom-call(f32[3,1,1,1440]{3,2,1,0:T(1,128)S(1)} %get-tuple-element.6.field_ref, f32[1,3]{1,0:T(1,128)S(1)} %get-tuple-element.7.table_ref), custom_call_target="tpu_custom_call" | custom-call | tf_op jit(solution)/shard_map/write_out/pallas_call | solution.py:318

commit v3 on v2

--- a/solution.py
+++ b/solution.py
@@ -34,15 +34,6 @@
     return pairs
 
 
-def other(me, k, n):
-    partner, bit = 0, 1
-    while bit < n:
-        here = (me // bit) % 2
-        partner = partner + bit * (1 - here if k & bit else here)
-        bit *= 2
-    return partner
-
-
 def steps(pair):
     return bin(pair).count("1")
 
@@ -99,7 +90,7 @@
 def kernel(
     n, nz, ens_ref, obs_ref, mask_ref, band_ref, field_ref, table_ref,
     ens_v, obs_v, mask_s, packet, obs_rows, gathered, partials,
-    load_sem, send_sem, recv_sem, share_sem, wave_sem,
+    load_sem, send_sem, recv_sem, share_sem, round_sem, wave_sem,
 ):
     held, variables, leads, rows, lon = ens_ref.shape
     units = variables * leads
@@ -110,12 +101,26 @@
     stride = obs_rows.shape[0] // n
     slots = n * held
     total = n * nz
+    chips = n // 2
+    depth = max(steps(pair) for pair in range(chips))
+    bits = [1 << b for b in range(depth)]
     me = lax.axis_index("member")
     band = lax.axis_index("lat")
     mine = band * n + me
     flag_line = packing.tails - 1
 
-    plane = [{"member": other(me, k, n), "lat": band} for k in range(1, n)]
+    rest, change, held_bit = me, {}, {}
+    for bit in [2 * bit for bit in bits[::-1]] + [1]:
+        held_bit[bit] = rest >= bit
+        change[bit] = jnp.where(held_bit[bit], -bit, bit)
+        rest = jnp.where(held_bit[bit], rest - bit, rest)
+    first_core = me - jnp.where(held_bit[1], 1, 0)
+
+    def beside(pair, c):
+        return first_core + sum(change[2 * bit] for bit in bits if pair & bit) + c
+
+    partner = me + change[1]
+    near = [beside(bit, c) for c in range(2) for bit in bits] + [partner]
     above = {"member": me, "lat": lax.rem(band + 1, nz)}
     below = {"member": me, "lat": lax.rem(band + nz - 1, nz)}
     has_above = band < nz - 1
@@ -124,14 +129,14 @@
     def signal(sem, peer):
         pl.semaphore_signal(sem, inc=1, device_id=peer, device_id_type=MESH)
 
-    barrier = pltpu.get_barrier_semaphore()
-    for peer in plane[::-1]:
-        signal(barrier, peer)
     mask_load = pltpu.make_async_copy(mask_ref, mask_s, load_sem.at[held + 1])
     ens_loads = [pltpu.make_async_copy(ens_ref.at[m], ens_v.at[m], load_sem.at[m]) for m in range(held)]
     obs_load = pltpu.make_async_copy(obs_ref, obs_v, load_sem.at[held])
     for load in [obs_load, mask_load] + ens_loads:
         load.start()
+    barrier = pltpu.get_barrier_semaphore()
+    for to in near:
+        signal(barrier, {"member": to, "lat": band})
     pl.when(has_above)(lambda: signal(barrier, above))
     pl.when(has_below)(lambda: signal(barrier, below))
 
@@ -163,7 +168,7 @@
     def send(chunk, to):
         low, size = layout.chunks[chunk]
         pltpu.make_async_remote_copy(
-            src_ref=packet.at[pl.ds(to * pitch + low, size)],
+            src_ref=packet.at[pl.ds(pl.multiple_of(to * pitch + low, SUBLANES), size)],
             dst_ref=gathered.at[pl.ds(pl.multiple_of(me * pitch + low, SUBLANES), size)],
             send_sem=send_sem,
             recv_sem=recv_sem.at[chunk],
@@ -171,18 +176,45 @@
             device_id_type=MESH,
         ).start()
 
+    def send_rows(pairs, cores, parts=(0, 1)):
+        for c in cores:
+            for pair in pairs:
+                for part in parts:
+                    send(part, beside(pair, c))
+
+    across, along = bits[: (depth + 1) // 2], bits[(depth + 1) // 2 :]
+
     for m in range(held):
         ens_loads[m].wait()
         pack(m, range(lines))
-    count_near = n - 1 + (band + nz - 1) // nz + (2 * nz - 2 - band) // nz
+    count_near = len(near) + (band + nz - 1) // nz + (2 * nz - 2 - band) // nz
     pl.semaphore_wait(barrier, count_near)
-    for to in sorted(range(n), key=lambda to: (-steps(to // 2), to)):
-
-        @pl.when(to != me)
-        def both(to=to):
-            send(0, to)
-            send(1, to)
-
+    def tell(far):
+        for bit in bits:
+            peer = me + change[2 * bit]
+            low_kept = jnp.logical_not(held_bit[2]) if bit == 1 else held_bit[2] | (peer < 2)
+            low_kept = low_kept | (peer < 2) if bit == 1 else low_kept
+            go = functools.partial(signal, round_sem.at[far - 2], {"member": peer, "lat": band})
+            if bit == bits[0]:
+                pl.when(low_kept)(go)
+            elif bit == bits[-1]:
+                pl.when(jnp.logical_not(low_kept))(go)
+            else:
+                go()
+
+    tell(2)
+    for c in range(2):
+        send_rows(across, [c], [0] if c else [0, 1])
+        send_rows(along, [c])
+    for far in range(2, depth + 1):
+        if far > 2:
+            tell(far)
+        else:
+            send(0, partner)
+            send(1, partner)
+        pl.semaphore_wait(round_sem.at[far - 2], depth - 1)
+        send_rows([pair for pair in range(chips) if steps(pair) == far], range(2))
+    send_rows(across, [1], [1])
     pl.when(band == nz - 1)(lambda: signal(wave_sem.at[1], below))
     for block in range(0, rows, SUBLANES):
         for line in range(lines):
@@ -204,7 +236,7 @@
     lane = lax.broadcasted_iota(jnp.int32, (SUBLANES, LANES), 1)
     below_line = lax.broadcasted_iota(jnp.int32, (SUBLANES, LANES), 0)
     sums = [None] * units
-    per_skill = per_spread = None
+    raw = []
     arrived(recv_sem.at[0], gathered, (n - 1) * layout.chunks[0][1])
     for j in range(0, lines, SUBLANES):
         if j == split:
@@ -217,10 +249,7 @@
             flags = functools.reduce(jnp.add, x)
             flags = jnp.where((below_line == flag_line) & free, flags, 0.0)
             count = jnp.max(jnp.max(flags, axis=0, keepdims=True), axis=1, keepdims=True)
-            count = jnp.broadcast_to(count, (SUBLANES, LANES))
-            per_one = 1.0 / count
-            per_spread = per_one / (count - 1.0)
-            per_skill = per_one + (slots - count) * per_spread
+            scale = 1.0 / (count * (count - 1.0))
         truth = obs_rows[pl.ds(pl.multiple_of(me * stride + j, SUBLANES), SUBLANES), :]
         skill = functools.reduce(jnp.add, [jnp.abs(value - truth) for value in x])
         for a, b in network:
@@ -229,11 +258,8 @@
             jnp.add,
             [(slots - 1.0 - 2.0 * i) * (x[slots - 1 - i] - x[i]) for i in range(slots // 2)],
         )
-        score = per_skill * skill - per_spread * spread
-        for u, low, wide, at, first in packing.pieces():
-            if j <= at < j + SUBLANES:
-                piece = score[at - j : at - j + 1, first : first + wide]
-                field_ref[u // leads, u % leads, :, pl.ds(low, wide)] = piece
+        score = (slots - 1.0) * skill - spread
+        raw.append(score)
         for u in range(units):
             part = jnp.where(packing.mask(u, below_line + j, lane), score, 0.0)
             sums[u] = part if sums[u] is None else sums[u] + part
@@ -243,23 +269,25 @@
     for u in range(units):
         one = jnp.sum(jnp.sum(sums[u], axis=0, keepdims=True), axis=1, keepdims=True)
         row = jnp.where(lane == u, one, row)
-    partials[pl.ds(mine, 1), :] = row * weight
+    partials[pl.ds(mine, 1), :] = row * (weight * scale)
 
     def share_with(far):
         return pltpu.make_async_remote_copy(
             src_ref=partials.at[pl.ds(mine, 1)],
             dst_ref=partials.at[pl.ds(mine, 1)],
-            send_sem=share_sem.at[0],
-            recv_sem=share_sem.at[1],
+            send_sem=send_sem,
+            recv_sem=share_sem,
             device_id={"member": far % n, "lat": far // n},
             device_id_type=MESH,
         )
 
     for far in range(total):
         pl.when(far != mine)(lambda far=far: share_with(far).start())
-    arrived(send_sem, packet, (n - 1) * held * lines)
-    arrived(share_sem.at[0], partials, total - 1)
-    arrived(share_sem.at[1], partials, total - 1)
+    for u, low, wide, at, first in packing.pieces():
+        piece = raw[at // SUBLANES][at % SUBLANES : at % SUBLANES + 1, first : first + wide]
+        field_ref[u // leads, u % leads, :, pl.ds(low, wide)] = piece * scale
+    arrived(send_sem, packet, (n - 1) * held * lines + total - 1)
+    arrived(share_sem, partials, total - 1)
     summed = jnp.sum(partials[...], axis=0, keepdims=True)
     table_ref[...] = summed[:, :units] / (nz * rows * lon)
 
@@ -283,6 +311,8 @@
     assert packing.tails and packing.used < LANES
     assert n % 2 == 0 and packing.lines >= 2 * SUBLANES
     pitch = Layout(held, packing.lines).pitch
+    depth = max(steps(pair) for pair in range(n // 2))
+    assert depth > 1 and n == 2 ** (depth + 1)
     stride = round_up(packing.lines, SUBLANES)
     total = n * nz
     field, table = pl.pallas_call(
@@ -307,7 +337,8 @@
             pltpu.SemaphoreType.DMA((held + 2,)),
             pltpu.SemaphoreType.DMA,
             pltpu.SemaphoreType.DMA((2,)),
-            pltpu.SemaphoreType.DMA((2,)),
+            pltpu.SemaphoreType.DMA,
+            pltpu.SemaphoreType.REGULAR((depth - 1,)),
             pltpu.SemaphoreType.REGULAR((2,)),
         ],
         compiler_params=pltpu.CompilerParams(

time: 16.6 us -> 16.4 us (0.988)
  Pallas kernels: 15.1 us -> 14.9 us
    pallas_call x1, Pallas kernels: 14.5 us -> 14.3 us  [on_device(): pl.pallas_call(functools.partial(kernel, n, nz), out_shape=(pltpu.VMEM((v...]
where the time goes in v3:
time: 16.4 us; the launch traced here: 16.2 us
  Pallas kernels  14.9 us (91%)
  between operations  1.28 us (8%)
    pallas_call x1, Pallas kernels, on_device(): pl.pallas_call(functools.partial(kernel, n, nz), out_shape=(pltpu.VMEM((v...  14.3 us
    pallas_call x1, Pallas kernels, on_device(): pl.pallas_call(write_out, out_shape=(jax.ShapeDtypeStruct(field.shape, jn...  0.63 us

profile of v3, /device:TPU:0, one launch (start us, length us, event | category | flops | bytes accessed | tf_op | source)
XLA Modules:
  0.0 16.2 jit_solution(11490074553635451807)
XLA Ops:
  1.3 14.3 %fair_crps.1 = (f32[3,1,1,1440]{3,2,1,0:T(1,128)S(1)}, f32[1,3]{1,0:T(1,128)S(1)}) custom-call(f32[2,3,1,8,1440]{4,3,2,1,0:T(8,128)} %ens_ref.1, f32[3,1,8,1440]{3,2,1,0:T(8,128)} %obs_ref.1, s32[2]{0:T(128)} %mask_ref.1, s32[1]{0:T(128)S(6)} %copy.6.band_ref), custom_call_target="tpu_custom_call" | custom-call | tf_op jit(solution)/shard_map/fair_crps/pallas_call | solution.py:318
  15.6 0.6 %write_out.1 = (f32[3,1,1,1440]{3,2,1,0:T(1,128)}, f32[1,3]{1,0:T(1,128)}) custom-call(f32[3,1,1,1440]{3,2,1,0:T(1,128)S(1)} %get-tuple-element.6.field_ref, f32[1,3]{1,0:T(1,128)S(1)} %get-tuple-element.7.table_ref), custom_call_target="tpu_custom_call" | custom-call | tf_op jit(solution)/shard_map/write_out/pallas_call | solution.py:349

commit v4 on v3

--- a/solution.py
+++ b/solution.py
@@ -76,20 +76,22 @@
 
 class Layout:
     def __init__(self, held, lines):
-        self.held, self.lines = held, lines
-        self.split = max(lines // SUBLANES - 1, 1) * SUBLANES
+        whole = lines // SUBLANES * SUBLANES
+        cuts = [0, whole - SUBLANES, whole, lines]
+        self.held, self.whole, self.moved = held, whole, lines - whole
         self.pitch = round_up(held * lines, SUBLANES)
-        self.chunks = [(0, held * self.split), (held * self.split, held * (lines - self.split))]
+        self.chunks = [(held * low, held * (high - low)) for low, high in zip(cuts, cuts[1:])]
+        self.lines = [(low, high - low) for low, high in zip(cuts, cuts[1:])]
 
     def row(self, m, line):
-        if line < self.split:
-            return m * self.split + line
-        return self.held * self.split + m * (self.lines - self.split) + line - self.split
+        for low, size in self.lines:
+            if line < low + size:
+                return self.held * low + m * size + line - low
 
 
 def kernel(
     n, nz, ens_ref, obs_ref, mask_ref, band_ref, field_ref, table_ref,
-    ens_v, obs_v, mask_s, packet, obs_rows, gathered, partials,
+    ens_v, obs_v, mask_s, packet, obs_rows, gathered, ends, sums, back, partials,
     load_sem, send_sem, recv_sem, share_sem, round_sem, wave_sem,
 ):
     held, variables, leads, rows, lon = ens_ref.shape
@@ -97,7 +99,7 @@
     packing = Packing(units, lon)
     lines = packing.lines
     layout = Layout(held, lines)
-    pitch, split = layout.pitch, layout.split
+    pitch, whole, moved = layout.pitch, layout.whole, layout.moved
     stride = obs_rows.shape[0] // n
     slots = n * held
     total = n * nz
@@ -176,11 +178,28 @@
             device_id_type=MESH,
         ).start()
 
+    def send_ends(to):
+        low, size = layout.chunks[2]
+        for which in range(2):
+            pltpu.make_async_remote_copy(
+                src_ref=packet.at[pl.ds(pl.multiple_of((to + 2 * which) * pitch + low, SUBLANES), size)],
+                dst_ref=ends.at[pl.ds(pl.multiple_of((2 * me + which) * SUBLANES, SUBLANES), size)],
+                send_sem=send_sem,
+                recv_sem=recv_sem.at[1],
+                device_id={"member": to, "lat": band},
+                device_id_type=MESH,
+            ).start()
+
     def send_rows(pairs, cores, parts=(0, 1)):
         for c in cores:
             for pair in pairs:
+                to = beside(pair, c)
                 for part in parts:
-                    send(part, beside(pair, c))
+                    send(part, to)
+                if 1 in parts:
+                    pl.when(held_bit[2] if pair % 2 else helps)(lambda: send_ends(to))
+
+    helps = jnp.logical_not(held_bit[2])
 
     across, along = bits[: (depth + 1) // 2], bits[(depth + 1) // 2 :]
 
@@ -203,28 +222,50 @@
                 go()
 
     tell(2)
-    for c in range(2):
-        send_rows(across, [c], [0] if c else [0, 1])
-        send_rows(along, [c])
+    toward = held_bit[2]
+    straight = held_bit[4]
+    send_rows(across, [0])
+    send_rows(along, [0])
+    pl.when((me < 2) | (straight & toward))(lambda: send_rows(across, [1], [0]))
+    pl.when(straight & toward)(lambda: send_rows(across, [1], [1]))
+    send_rows(along, [1])
     for far in range(2, depth + 1):
         if far > 2:
             tell(far)
         else:
             send(0, partner)
             send(1, partner)
+            pl.when(helps)(lambda: send_ends(partner))
         pl.semaphore_wait(round_sem.at[far - 2], depth - 1)
-        send_rows([pair for pair in range(chips) if steps(pair) == far], range(2))
-    send_rows(across, [1], [1])
+        diagonal = [pair for pair in range(chips) if steps(pair) == far]
+        send_rows(diagonal, [0])
+        if far == 2:
+            pl.when(straight & jnp.logical_not(toward))(lambda: send_rows(across, [1], [0]))
+        send_rows(diagonal, [1])
+    pl.when(toward & jnp.logical_not(straight))(lambda: send_rows(across, [1], [0]))
+    pl.when(jnp.logical_not(straight & toward))(lambda: send_rows(across, [1], [1]))
     pl.when(band == nz - 1)(lambda: signal(wave_sem.at[1], below))
     for block in range(0, rows, SUBLANES):
         for line in range(lines):
             obs_rows[pl.ds(block * stride + line, SUBLANES, stride=stride), :] = obs_line(block, line)
     own = pl.ds(pl.multiple_of(me * pitch, SUBLANES), pitch)
     gathered[own, :] = packet[own, :]
+
+    @pl.when(helps)
+    def _():
+        low, size = layout.chunks[2]
+        for which in range(2):
+            mine_at = pl.ds(pl.multiple_of((2 * me + which) * SUBLANES, SUBLANES), size)
+            ends[mine_at, :] = packet[pl.ds(pl.multiple_of((me + 2 * which) * pitch + low, SUBLANES), size), :]
+
     pl.when(has_below)(lambda: pl.semaphore_wait(wave_sem.at[0], 1))
     pl.when(has_above)(lambda: signal(wave_sem.at[0], above))
-    row_number = jnp.full((1, LANES), band_ref[0] + me, jnp.int32).astype(jnp.float32)
-    weight = jnp.cos((90.0 - row_number * 180.0 / (GRID_LAT - 1)) * math.pi / 180.0)
+
+    def weight_of(row):
+        number = jnp.full((1, LANES), band_ref[0] + row, jnp.int32).astype(jnp.float32)
+        return jnp.cos((90.0 - number * 180.0 / (GRID_LAT - 1)) * math.pi / 180.0)
+
+    weight, other_weight = weight_of(me), weight_of(me + 2)
     pl.when(has_above)(lambda: pl.semaphore_wait(wave_sem.at[1], 1))
     pl.when(has_above & has_below)(lambda: signal(wave_sem.at[1], below))
 
@@ -235,12 +276,34 @@
     network = sort_pairs(slots)
     lane = lax.broadcasted_iota(jnp.int32, (SUBLANES, LANES), 1)
     below_line = lax.broadcasted_iota(jnp.int32, (SUBLANES, LANES), 0)
-    sums = [None] * units
     raw = []
+
+    def crps(x, truth):
+        x = list(x)
+        skill = functools.reduce(jnp.add, [jnp.abs(value - truth) for value in x])
+        for a, b in network:
+            x[a], x[b] = jnp.minimum(x[a], x[b]), jnp.maximum(x[a], x[b])
+        spread = functools.reduce(
+            jnp.add,
+            [(slots - 1.0 - 2.0 * i) * (x[slots - 1 - i] - x[i]) for i in range(slots // 2)],
+        )
+        return (slots - 1.0) * skill - spread
+
+    def by_unit(score, line):
+        return [jnp.where(packing.mask(u, line, lane), score, 0.0) for u in range(units)]
+
+    def put(score, j, size):
+        for u, low, wide, at, first in packing.pieces():
+            if j <= at < j + size:
+                field_ref[u // leads, u % leads, :, pl.ds(low, wide)] = score[at - j : at - j + 1, first : first + wide]
+
     arrived(recv_sem.at[0], gathered, (n - 1) * layout.chunks[0][1])
-    for j in range(0, lines, SUBLANES):
-        if j == split:
-            arrived(recv_sem.at[1], gathered, (n - 1) * layout.chunks[1][1])
+    parts = None
+    for j in range(0, whole, SUBLANES):
+        if j == layout.lines[1][0]:
+            late, end = (n - 1) * layout.chunks[1][1], 2 * (n - 1) * layout.chunks[2][1]
+            pl.when(helps)(lambda: arrived(recv_sem.at[1], gathered, late + end))
+            pl.when(held_bit[2])(lambda: arrived(recv_sem.at[1], gathered, late))
         x = [
             gathered[pl.ds(s // held * pitch + layout.row(s % held, j), SUBLANES), :]
             for s in range(slots)
@@ -250,26 +313,38 @@
             flags = jnp.where((below_line == flag_line) & free, flags, 0.0)
             count = jnp.max(jnp.max(flags, axis=0, keepdims=True), axis=1, keepdims=True)
             scale = 1.0 / (count * (count - 1.0))
-        truth = obs_rows[pl.ds(pl.multiple_of(me * stride + j, SUBLANES), SUBLANES), :]
-        skill = functools.reduce(jnp.add, [jnp.abs(value - truth) for value in x])
-        for a, b in network:
-            x[a], x[b] = jnp.minimum(x[a], x[b]), jnp.maximum(x[a], x[b])
-        spread = functools.reduce(
-            jnp.add,
-            [(slots - 1.0 - 2.0 * i) * (x[slots - 1 - i] - x[i]) for i in range(slots // 2)],
+        raw.append(crps(x, obs_rows[pl.ds(pl.multiple_of(me * stride + j, SUBLANES), SUBLANES), :]))
+        more = by_unit(raw[-1], below_line + j)
+        parts = more if parts is None else [a + b for a, b in zip(parts, more)]
+    for u in range(units):
+        sums[u] = parts[u] * weight
+
+    @pl.when(helps)
+    def _():
+        upper = below_line < moved
+        x = []
+        for s in range(slots):
+            at = s // held * 2 * SUBLANES + s % held * moved
+            mine_here = ends[pl.ds(at, SUBLANES), :]
+            x.append(jnp.where(upper, mine_here, ends[pl.ds(at + SUBLANES - moved, SUBLANES), :]))
+        truth = jnp.where(
+            upper,
+            obs_rows[pl.ds(me * stride + whole, SUBLANES), :],
+            obs_rows[pl.ds((me + 2) * stride + whole - moved, SUBLANES), :],
         )
-        score = (slots - 1.0) * skill - spread
-        raw.append(score)
-        for u in range(units):
-            part = jnp.where(packing.mask(u, below_line + j, lane), score, 0.0)
-            sums[u] = part if sums[u] is None else sums[u] + part
+        score = crps(x, truth)
+        back[pl.ds(0, SUBLANES), :] = score
+        weighed = jnp.where(below_line < 2 * moved, score, 0.0) * jnp.where(upper, weight, other_weight)
+        line = jnp.where(upper, below_line, below_line - moved) + whole
+        for u, part in enumerate(by_unit(weighed, line)):
+            sums[u] += part
 
     lane = lax.broadcasted_iota(jnp.int32, (1, LANES), 1)
     row = jnp.zeros((1, LANES), jnp.float32)
     for u in range(units):
         one = jnp.sum(jnp.sum(sums[u], axis=0, keepdims=True), axis=1, keepdims=True)
         row = jnp.where(lane == u, one, row)
-    partials[pl.ds(mine, 1), :] = row * (weight * scale)
+    partials[pl.ds(mine, 1), :] = row * scale
 
     def share_with(far):
         return pltpu.make_async_remote_copy(
@@ -283,11 +358,31 @@
 
     for far in range(total):
         pl.when(far != mine)(lambda far=far: share_with(far).start())
-    for u, low, wide, at, first in packing.pieces():
-        piece = raw[at // SUBLANES][at % SUBLANES : at % SUBLANES + 1, first : first + wide]
-        field_ref[u // leads, u % leads, :, pl.ds(low, wide)] = piece * scale
-    arrived(send_sem, packet, (n - 1) * held * lines + total - 1)
-    arrived(share_sem, partials, total - 1)
+    give_back = pltpu.make_async_remote_copy(
+        src_ref=back.at[pl.ds(0, SUBLANES)],
+        dst_ref=back.at[pl.ds(SUBLANES, SUBLANES)],
+        send_sem=send_sem,
+        recv_sem=share_sem,
+        device_id={"member": me + change[2], "lat": band},
+        device_id_type=MESH,
+    )
+    pl.when(helps)(lambda: give_back.start())
+    for j, score in enumerate(raw):
+        put(score * scale, j * SUBLANES, SUBLANES)
+    sent = (n - 1) * held * whole + total - 1
+
+    @pl.when(helps)
+    def _():
+        put(back[pl.ds(0, SUBLANES), :] * scale, whole, moved)
+        arrived(send_sem, packet, sent + (n - 2) * layout.chunks[2][1] + SUBLANES)
+        arrived(share_sem, packet, total - 1)
+
+    @pl.when(held_bit[2])
+    def _():
+        arrived(send_sem, packet, sent + n * layout.chunks[2][1])
+        arrived(share_sem, packet, total - 1 + SUBLANES)
+        put(back[pl.ds(SUBLANES + moved, SUBLANES), :] * scale, whole, moved)
+
     summed = jnp.sum(partials[...], axis=0, keepdims=True)
     table_ref[...] = summed[:, :units] / (nz * rows * lon)
 
@@ -309,11 +404,13 @@
     units = variables * leads
     packing = Packing(units, lon)
     assert packing.tails and packing.used < LANES
-    assert n % 2 == 0 and packing.lines >= 2 * SUBLANES
-    pitch = Layout(held, packing.lines).pitch
+    layout = Layout(held, packing.lines)
+    assert packing.lines >= 2 * SUBLANES and 0 < layout.moved <= SUBLANES // 2
+    assert held * layout.moved <= SUBLANES and held * layout.whole % SUBLANES == 0
+    pitch = layout.pitch
     depth = max(steps(pair) for pair in range(n // 2))
     assert depth > 1 and n == 2 ** (depth + 1)
-    stride = round_up(packing.lines, SUBLANES)
+    stride = round_up(packing.lines + SUBLANES, SUBLANES)
     total = n * nz
     field, table = pl.pallas_call(
         functools.partial(kernel, n, nz),
@@ -333,6 +430,9 @@
             pltpu.VMEM((n * pitch, LANES), jnp.float32),
             pltpu.VMEM((n * stride, LANES), jnp.float32),
             pltpu.VMEM((n * pitch + SUBLANES, LANES), jnp.float32),
+            pltpu.VMEM((2 * n * SUBLANES + SUBLANES, LANES), jnp.float32),
+            pltpu.VMEM((units, SUBLANES, LANES), jnp.float32),
+            pltpu.VMEM((3 * SUBLANES, LANES), jnp.float32),
             pltpu.VMEM((total, LANES), jnp.float32),
             pltpu.SemaphoreType.DMA((held + 2,)),
             pltpu.SemaphoreType.DMA,

time: 16.4 us -> 16.3 us (level)
  no operation moved by 1% of the time
where the time goes in v4:
time: 16.3 us; the launch traced here: 16.1 us
  Pallas kernels  14.8 us (91%)
  between operations  1.28 us (8%)
    pallas_call x1, Pallas kernels, on_device(): pl.pallas_call(functools.partial(kernel, n, nz), out_shape=(pltpu.VMEM((v...  14.2 us
    pallas_call x1, Pallas kernels, on_device(): pl.pallas_call(write_out, out_shape=(jax.ShapeDtypeStruct(field.shape, jn...  0.63 us

profile of v4, /device:TPU:0, one launch (start us, length us, event | category | flops | bytes accessed | tf_op | source)
XLA Modules:
  0.0 16.1 jit_solution(17781565227766459912)
XLA Ops:
  1.3 14.2 %fair_crps.1 = (f32[3,1,1,1440]{3,2,1,0:T(1,128)S(1)}, f32[1,3]{1,0:T(1,128)S(1)}) custom-call(f32[2,3,1,8,1440]{4,3,2,1,0:T(8,128)} %ens_ref.1, f32[3,1,8,1440]{3,2,1,0:T(8,128)} %obs_ref.1, s32[2]{0:T(128)} %mask_ref.1, s32[1]{0:T(128)S(6)} %copy.6.band_ref), custom_call_target="tpu_custom_call" | custom-call | tf_op jit(solution)/shard_map/fair_crps/pallas_call | solution.py:415
  15.5 0.6 %write_out.1 = (f32[3,1,1,1440]{3,2,1,0:T(1,128)}, f32[1,3]{1,0:T(1,128)}) custom-call(f32[3,1,1,1440]{3,2,1,0:T(1,128)S(1)} %get-tuple-element.6.field_ref, f32[1,3]{1,0:T(1,128)S(1)} %get-tuple-element.7.table_ref), custom_call_target="tpu_custom_call" | custom-call | tf_op jit(solution)/shard_map/write_out/pallas_call | solution.py:449
